TPU v7x, 32 devices: a whole 2x2x4 slice. The times are simulated.
32 devices in a mesh: dp: 8 (over y, x, core), tensor: 4 (over z).
Axes of the slice: x: 2, y: 2, z: 4, core: 2. Of those that a mesh axis runs over, the one named last changes fastest.
Arguments:
- inputs: bfloat16 [4, 4096, 768], P(None, ('dp', 'tensor')), may hold values from -12 to 12
- cotangent: bfloat16 [4, 4096, 768], P(None, ('dp', 'tensor')), may hold values from -12 to 12
- segment_ids: int32 [4, 8, 512], P(None, 'dp'), may hold values from 0 to 23, never falling along the last dimension, each value on 1 to 48 neighbouring positions
- ln1_gain: float32 [768], replicated, may hold values from 0.25 to 1.75
- ln1_bias: float32 [768], replicated, may hold values from -1.75 to 1.75
- qkv_weight: bfloat16 [3, 768, 768], P(None, 'dp', 'tensor'), may hold values from -0.21875 to 0.21875
- qv_bias: float32 [2, 768], P(None, 'tensor'), may hold values from -1.75 to 1.75
- out_weight: bfloat16 [768, 768], P('tensor', 'dp'), may hold values from -0.4375 to 0.4375
- out_bias: float32 [768], replicated, may hold values from -1.75 to 1.75
- ln2_gain: float32 [768], replicated, may hold values from 0.25 to 1.75
- ln2_bias: float32 [768], replicated, may hold values from -1.75 to 1.75
- up_weight: bfloat16 [768, 3072], P('dp', 'tensor'), may hold values from -0.21875 to 0.21875
- up_bias: float32 [3072], P('tensor'), may hold values from -1.75 to 1.75
- down_weight: bfloat16 [3072, 768], P('tensor', 'dp'), may hold values from -0.109375 to 0.109375
- down_bias: float32 [768], replicated, may hold values from -1.75 to 1.75
Outputs:
- outputs: float32 [4, 4096, 768], P(None, ('dp', 'tensor'))
- input_grad: float32 [4, 4096, 768], P(None, ('dp', 'tensor'))
- ln1_gain_grad: float32 [768], replicated
- ln1_bias_grad: float32 [768], replicated
- qkv_weight_grad: float32 [3, 768, 768], P(None, 'dp', 'tensor')
- qv_bias_grad: float32 [2, 768], replicated
- out_weight_grad: float32 [768, 768], P('tensor', 'dp')
- out_bias_grad: float32 [768], replicated
- ln2_gain_grad: float32 [768], replicated
- ln2_bias_grad: float32 [768], replicated
- up_weight_grad: float32 [768, 3072], P('dp', 'tensor')
- up_bias_grad: float32 [3072], replicated
- down_weight_grad: float32 [3072, 768], P('tensor', 'dp')
- down_bias_grad: float32 [768], replicated
Inputs may be any that keep to these rules, and one draw needn't show every extreme that they name: `segment_ids`: along each sequence of 512 tokens the ids never fall; a caption spans 1 to 48 tokens, and one caption of each sequence exactly 48.
All inputs are finite; a program needn't handle non-finite values.
Results may differ from a plain program's by a relative error of at most 0.017.
Values may be sent and summed in bfloat16 or wider, within the bound.
A program may use at most 192 MiB of HBM per device.

v0:
```python
import jax
import jax.numpy as jnp
from jax import lax
from jax.sharding import PartitionSpec as P

HD = 64
epsilon = 1e-05
masked_value = -1000000000.0


def layer_norm(stream_values, scales, shifts):
    centered = stream_values - jnp.mean(stream_values, -1, keepdims=True)
    variance = jnp.mean(centered * centered, -1, keepdims=True)
    return centered * lax.rsqrt(variance + epsilon) * scales + shifts


def gelu_exact(hidden):
    return jax.nn.gelu(hidden, approximate=False)


def contract(operand_left, operand_right, left_dim, right_dim):
    return lax.dot_general(
        operand_left,
        operand_right,
        (((left_dim,), (right_dim,)), ((), ())),
        preferred_element_type=jnp.float32,
    )


def gather_rows(values_low):
    return lax.all_gather(values_low, "tensor", axis=0, tiled=True)


def gather_grads(values_low):
    return lax.all_gather(values_low, "tensor", axis=0, tiled=True)


def rows_sum(operand_left, operand_right, einsum_form):
    return lax.psum_scatter(
        jnp.einsum(
            einsum_form, operand_left, operand_right, preferred_element_type=jnp.float32
        ).astype(jnp.bfloat16),
        "tensor",
        scatter_dimension=0,
        tiled=True,
    ).astype(jnp.float32)


def grads_sum(operand_left, operand_right, einsum_form):
    return lax.psum_scatter(
        jnp.einsum(
            einsum_form, operand_left, operand_right, preferred_element_type=jnp.float32
        ).astype(jnp.bfloat16),
        "tensor",
        scatter_dimension=0,
        tiled=True,
    ).astype(jnp.float32)


def scores_of(query_heads, key_heads, same_caption):
    raw_scores = jnp.einsum(
        "bqhd,bkhd->bhqk", query_heads, key_heads, preferred_element_type=jnp.float32
    )
    return jnp.where(same_caption, raw_scores * HD ** (-0.5), masked_value)


def body(
    inputs,
    cotangent,
    segment_ids,
    ln1_gain,
    ln1_bias,
    qkv_weight,
    qv_bias,
    out_weight,
    out_bias,
    ln2_gain,
    ln2_bias,
    up_weight,
    up_bias,
    down_weight,
    down_bias,
):
    batches, shard_rows, model_width = inputs.shape
    sequences, seq_length = (segment_ids.shape[1], segment_ids.shape[2])
    head_cols = qkv_weight.shape[2]
    local_heads = head_cols // HD
    hidden_local = up_weight.shape[1]
    full_rows = sequences * seq_length
    shape_heads = (sequences, seq_length, local_heads, HD)
    tensor_pos = lax.axis_index("tensor")
    zero_index = tensor_pos * 0
    full_grads = (
        jnp.zeros((3, model_width, head_cols), jnp.float32),
        jnp.zeros((head_cols, model_width), jnp.float32),
        jnp.zeros((model_width, hidden_local), jnp.float32),
        jnp.zeros((hidden_local, model_width), jnp.float32),
    )
    qv_total = jnp.zeros((2, head_cols), jnp.float32)
    up_total = jnp.zeros((hidden_local,), jnp.float32)
    out_total = jnp.zeros((model_width,), jnp.float32)
    down_total = jnp.zeros((model_width,), jnp.float32)
    gain1_total = jnp.zeros((model_width,), jnp.float32)
    shift1_total = jnp.zeros((model_width,), jnp.float32)
    gain2_total = jnp.zeros((model_width,), jnp.float32)
    shift2_total = jnp.zeros((model_width,), jnp.float32)
    result_list = []
    input_list = []
    for micro_index in range(batches):
        weights_now = (
            lax.all_gather(qkv_weight, "dp", axis=1, tiled=True),
            lax.all_gather(out_weight, "dp", axis=1, tiled=True),
            lax.all_gather(up_weight, "dp", axis=0, tiled=True),
            lax.all_gather(down_weight, "dp", axis=1, tiled=True),
        )
        qkv_full, out_full, up_full, down_full = weights_now
        segment_now = segment_ids[micro_index]
        same_caption = (segment_now[:, :, None] == segment_now[:, None, :])[:, None]
        stream = inputs[micro_index].astype(jnp.float32)
        normed, norm_pull = jax.vjp(layer_norm, stream, ln1_gain, ln1_bias)
        normed_rows = gather_rows(normed.astype(jnp.bfloat16))
        query_heads = (
            (contract(normed_rows, qkv_full[0], 1, 0) + qv_bias[0])
            .astype(jnp.bfloat16)
            .reshape(shape_heads)
        )
        key_heads = (
            contract(normed_rows, qkv_full[1], 1, 0).astype(jnp.bfloat16).reshape(shape_heads)
        )
        value_heads = (
            (contract(normed_rows, qkv_full[2], 1, 0) + qv_bias[1])
            .astype(jnp.bfloat16)
            .reshape(shape_heads)
        )
        scores = scores_of(query_heads, key_heads, same_caption)
        row_top = jnp.max(scores, -1, keepdims=True)
        shifted = jnp.exp(scores - row_top)
        row_total = jnp.sum(shifted, -1, keepdims=True)
        log_total = row_top + jnp.log(row_total)
        probs_low = (shifted / row_total).astype(jnp.bfloat16)
        mixed = jnp.einsum(
            "bhqk,bkhd->bqhd", probs_low, value_heads, preferred_element_type=jnp.float32
        )
        mixed = mixed.reshape(full_rows, head_cols).astype(jnp.bfloat16)
        middle = stream + rows_sum(mixed, out_full, "sc,cd->sd") + out_bias
        normed_two, norm_two_pull = jax.vjp(layer_norm, middle, ln2_gain, ln2_bias)
        normed_two_rows = gather_rows(normed_two.astype(jnp.bfloat16))
        hidden = contract(normed_two_rows, up_full, 1, 0) + up_bias
        active, gelu_pull = jax.vjp(gelu_exact, hidden)
        active_low = active.astype(jnp.bfloat16)
        feed_out = rows_sum(active_low, down_full, "sc,cd->sd") + down_bias
        result_list.append(middle + feed_out)
        grad_stream = cotangent[micro_index].astype(jnp.float32)
        feed_grad = cotangent[micro_index]
        down_total = down_total + jnp.sum(feed_grad.astype(jnp.float32), 0)
        feed_rows = gather_grads(feed_grad)
        grad_down = contract(active_low, feed_rows, 0, 0)
        hidden_grad = gelu_pull(contract(feed_rows, down_full, 1, 1))[0].astype(jnp.bfloat16)
        up_total = up_total + jnp.sum(hidden_grad.astype(jnp.float32), 0)
        grad_up = contract(normed_two_rows, hidden_grad, 0, 0)
        normed_two_grad = grads_sum(hidden_grad, up_full, "sc,dc->sd")
        middle_part, gain2_grad, shift2_grad = norm_two_pull(normed_two_grad)
        gain2_total = gain2_total + gain2_grad
        shift2_total = shift2_total + shift2_grad
        middle_grad = grad_stream + middle_part
        branch_grad = middle_grad.astype(jnp.bfloat16)
        out_total = out_total + jnp.sum(branch_grad.astype(jnp.float32), 0)
        branch_rows = gather_grads(branch_grad)
        grad_out = contract(mixed, branch_rows, 0, 0)
        mixed_grad = contract(branch_rows, out_full, 1, 1).astype(jnp.bfloat16).reshape(shape_heads)
        attention = jnp.exp(scores_of(query_heads, key_heads, same_caption) - log_total)
        probs_grad = jnp.einsum(
            "bqhd,bkhd->bhqk", mixed_grad, value_heads, preferred_element_type=jnp.float32
        )
        value_grad = jnp.einsum(
            "bhqk,bqhd->bkhd",
            attention.astype(jnp.bfloat16),
            mixed_grad,
            preferred_element_type=jnp.float32,
        )
        scores_grad = attention * (probs_grad - jnp.sum(attention * probs_grad, -1, keepdims=True))
        scores_grad = scores_grad.astype(jnp.bfloat16)
        query_grad = jnp.einsum(
            "bhqk,bkhd->bqhd", scores_grad, key_heads, preferred_element_type=jnp.float32
        ) * HD ** (-0.5)
        key_grad = jnp.einsum(
            "bhqk,bqhd->bkhd", scores_grad, query_heads, preferred_element_type=jnp.float32
        ) * HD ** (-0.5)
        grad_project = jnp.stack(
            [
                query_grad.reshape(full_rows, head_cols),
                key_grad.reshape(full_rows, head_cols),
                value_grad.reshape(full_rows, head_cols),
            ],
            1,
        ).astype(jnp.bfloat16)
        qv_total = qv_total + jnp.sum(grad_project[:, 0::2].astype(jnp.float32), 0)
        grad_qkv = jnp.einsum(
            "sd,sjc->jdc", normed_rows, grad_project, preferred_element_type=jnp.float32
        )
        normed_grad = grads_sum(grad_project, qkv_full, "sjc,jdc->sd")
        stream_part, gain1_grad, shift1_grad = norm_pull(normed_grad)
        gain1_total = gain1_total + gain1_grad
        shift1_total = shift1_total + shift1_grad
        input_list.append(middle_grad + stream_part)
        full_grads = jax.tree.map(jnp.add, full_grads, (grad_qkv, grad_out, grad_up, grad_down))
    qkv_share, out_share, up_share, down_share = (
        lax.psum_scatter(full_grads[0], "dp", scatter_dimension=1, tiled=True),
        lax.psum_scatter(full_grads[1], "dp", scatter_dimension=1, tiled=True),
        lax.psum_scatter(full_grads[2], "dp", scatter_dimension=0, tiled=True),
        lax.psum_scatter(full_grads[3], "dp", scatter_dimension=1, tiled=True),
    )
    qv_whole = lax.dynamic_update_slice(
        jnp.zeros((2, model_width), jnp.float32), qv_total, (zero_index, tensor_pos * head_cols)
    )
    up_whole = lax.dynamic_update_slice(
        jnp.zeros((hidden_local * lax.axis_size("tensor"),), jnp.float32),
        up_total,
        (tensor_pos * hidden_local,),
    )
    summed = lax.psum(
        (
            qv_whole,
            up_whole,
            out_total,
            down_total,
            gain1_total,
            shift1_total,
            gain2_total,
            shift2_total,
        ),
        ("dp", "tensor"),
    )
    qv_sum, up_sum, out_sum, down_sum, gain1_sum, shift1_sum, gain2_sum, shift2_sum = summed
    return (
        jnp.stack(result_list),
        jnp.stack(input_list),
        gain1_sum,
        shift1_sum,
        qkv_share,
        qv_sum,
        out_share,
        out_sum,
        gain2_sum,
        shift2_sum,
        up_share,
        up_sum,
        down_share,
        down_sum,
    )


def solution(mesh):
    in_specs = (
        P(None, ("dp", "tensor"), None),
        P(None, ("dp", "tensor"), None),
        P(None, "dp", None),
        P(),
        P(),
        P(None, "dp", "tensor"),
        P(None, "tensor"),
        P("tensor", "dp"),
        P(),
        P(),
        P(),
        P("dp", "tensor"),
        P("tensor"),
        P("tensor", "dp"),
        P(),
    )
    out_specs = (
        P(None, ("dp", "tensor"), None),
        P(None, ("dp", "tensor"), None),
        P(),
        P(),
        P(None, "dp", "tensor"),
        P(),
        P("tensor", "dp"),
        P(),
        P(),
        P(),
        P("dp", "tensor"),
        P(),
        P("tensor", "dp"),
        P(),
    )
    return jax.shard_map(body, mesh=mesh, in_specs=in_specs, out_specs=out_specs, check_vma=False)
```

profile of v0, /device:TPU:0, one launch (start us, length us, event | category | flops | bytes accessed | tf_op | source)
XLA Modules:
  0.0 885.6 jit_solution(6010277338871002044)
XLA Ops:
  11.8 21.3 %all_gather.72 = bf16[512,768]{1,0:T(8,128)(2,1)S(1)} all-gather(bf16[128,768]{1,0:T(8,128)(2,1)S(1)} %fusion.157), channel_id=1, replica_groups=mesh['dp'=8,'tensor'=4] {'tensor'}, dimensions={0}, use_global_device_ids=true | all-gather | bytes 983040 | tf_op jit(solution)/shard_map/all_gather | solution.py:31
  61.0 21.4 %reduce-scatter.25.cloned.1.call-done = bf16[128,768]{1,0:T(8,128)(2,1)} async-done(((bf16[512,768]{1,0:T(8,128)(2,1)}), bf16[128,768]{1,0:T(8,128)(2,1)}) %reduce-scatter.25.cloned.1.call-update) | async-done | bytes 196624 | tf_op jit(solution)/shard_map/reduce_scatter | solution.py:39
  83.8 17.9 %all_gather.80 = bf16[512,768]{1,0:T(8,128)(2,1)S(1)} all-gather(bf16[128,768]{1,0:T(8,128)(2,1)S(1)} %fusion.153), channel_id=1, replica_groups=mesh['dp'=8,'tensor'=4] {'tensor'}, dimensions={0}, use_global_device_ids=true | all-gather | bytes 983040 | tf_op jit(solution)/shard_map/all_gather | solution.py:31
  110.3 27.7 %all-gather.2 = bf16[1,512,768]{2,1,0:T(8,128)(2,1)} all-gather(bf16[1,128,768]{2,1,0:T(8,128)(2,1)S(1)} %get-tuple-element.151), channel_id=4, replica_groups=mesh['dp'=8,'tensor'=4] {'tensor'}, dimensions={1}, use_global_device_ids=true | all-gather | bytes 983040 | tf_op jit(solution)/shard_map/all_gather | solution.py:35
  137.9 18.3 %all-gather = bf16[1,512,768]{2,1,0:T(8,128)(2,1)} all-gather(bf16[1,128,768]{2,1,0:T(8,128)(2,1)S(1)} %get-tuple-element.149), channel_id=2, replica_groups=mesh['dp'=8,'tensor'=4] {'tensor'}, dimensions={1}, use_global_device_ids=true | all-gather | bytes 983040 | tf_op jit(solution)/shard_map/all_gather | solution.py:35
  163.2 20.1 %all_gather.78 = bf16[512,768]{1,0:T(8,128)(2,1)S(1)} all-gather(bf16[128,768]{1,0:T(8,128)(2,1)S(1)} %get-tuple-element.141), channel_id=1, replica_groups=mesh['dp'=8,'tensor'=4] {'tensor'}, dimensions={0}, use_global_device_ids=true | all-gather | bytes 983040 | tf_op jit(solution)/shard_map/all_gather | solution.py:31
  214.8 22.9 %all_gather.75 = bf16[512,768]{1,0:T(8,128)(2,1)S(1)} all-gather(bf16[128,768]{1,0:T(8,128)(2,1)S(1)} %copy-done.129), channel_id=1, replica_groups=mesh['dp'=8,'tensor'=4] {'tensor'}, dimensions={0}, use_global_device_ids=true | all-gather | bytes 983040 | tf_op jit(solution)/shard_map/all_gather | solution.py:31
  253.8 27.9 %all_gather.82 = bf16[512,768]{1,0:T(8,128)(2,1)S(1)} all-gather(bf16[128,768]{1,0:T(8,128)(2,1)S(1)} %copy-done.128), channel_id=1, replica_groups=mesh['dp'=8,'tensor'=4] {'tensor'}, dimensions={0}, use_global_device_ids=true | all-gather | bytes 983040 | tf_op jit(solution)/shard_map/all_gather | solution.py:31
  293.1 22.7 %all-gather.3 = bf16[1,512,768]{2,1,0:T(8,128)(2,1)} all-gather(bf16[1,128,768]{2,1,0:T(8,128)(2,1)S(1)} %copy-done.107), channel_id=5, replica_groups=mesh['dp'=8,'tensor'=4] {'tensor'}, dimensions={1}, use_global_device_ids=true | all-gather | bytes 983040 | tf_op jit(solution)/shard_map/all_gather | solution.py:35
  315.8 24.3 %all-gather.1 = bf16[1,512,768]{2,1,0:T(8,128)(2,1)} all-gather(bf16[1,128,768]{2,1,0:T(8,128)(2,1)S(1)} %copy-done.106), channel_id=3, replica_groups=mesh['dp'=8,'tensor'=4] {'tensor'}, dimensions={1}, use_global_device_ids=true | all-gather | bytes 983040 | tf_op jit(solution)/shard_map/all_gather | solution.py:35
  347.5 19.9 %reduce-scatter.27.cloned.1.call-done = bf16[128,768]{1,0:T(8,128)(2,1)} async-done(((bf16[512,768]{1,0:T(8,128)(2,1)}), bf16[128,768]{1,0:T(8,128)(2,1)}) %reduce-scatter.27.cloned.1.call-update) | async-done | bytes 196624 | tf_op jit(solution)/shard_map/reduce_scatter | solution.py:39
  371.4 27.1 %all_gather.83 = bf16[512,768]{1,0:T(8,128)(2,1)S(1)} all-gather(bf16[128,768]{1,0:T(8,128)(2,1)S(1)} %get-tuple-element.137), channel_id=1, replica_groups=mesh['dp'=8,'tensor'=4] {'tensor'}, dimensions={0}, use_global_device_ids=true | all-gather | bytes 983040 | tf_op jit(solution)/shard_map/all_gather | solution.py:31
  408.8 19.2 %all_gather.79 = bf16[512,768]{1,0:T(8,128)(2,1)} all-gather(bf16[128,768]{1,0:T(8,128)(2,1)} %get-tuple-element.136), channel_id=1, replica_groups=mesh['dp'=8,'tensor'=4] {'tensor'}, dimensions={0}, use_global_device_ids=true | all-gather | bytes 983040 | tf_op jit(solution)/shard_map/all_gather | solution.py:31
  432.1 25.1 %all_gather.89 = bf16[512,768]{1,0:T(8,128)(2,1)S(1)} all-gather(bf16[128,768]{1,0:T(8,128)(2,1)S(1)} %get-tuple-element.109), channel_id=1, replica_groups=mesh['dp'=8,'tensor'=4] {'tensor'}, dimensions={0}, use_global_device_ids=true | all-gather | bytes 983040 | tf_op jit(solution)/shard_map/all_gather | solution.py:35
  491.7 25.0 %reduce-scatter.51.cloned.1.call-done = bf16[128,768]{1,0:T(8,128)(2,1)} async-done(((bf16[512,768]{1,0:T(8,128)(2,1)}), bf16[128,768]{1,0:T(8,128)(2,1)}) %reduce-scatter.51.cloned.1.call-update) | async-done | bytes 196624 | tf_op jit(solution)/shard_map/reduce_scatter | solution.py:50
  519.6 22.0 %reduce-scatter.31.cloned.1.call-done = bf16[128,768]{1,0:T(8,128)(2,1)} async-done(((bf16[512,768]{1,0:T(8,128)(2,1)}), bf16[128,768]{1,0:T(8,128)(2,1)}) %reduce-scatter.31.cloned.1.call-update) | async-done | bytes 196624 | tf_op jit(solution)/shard_map/reduce_scatter | solution.py:39
  543.8 22.8 %reduce-scatter.39.cloned.1.call-done = bf16[128,768]{1,0:T(8,128)(2,1)} async-done(((bf16[512,768]{1,0:T(8,128)(2,1)}), bf16[128,768]{1,0:T(8,128)(2,1)}) %reduce-scatter.39.cloned.1.call-update) | async-done | bytes 196624 | tf_op jit(solution)/shard_map/reduce_scatter | solution.py:39
  569.6 18.4 %all_gather.85 = bf16[512,768]{1,0:T(8,128)(2,1)S(1)} all-gather(bf16[128,768]{1,0:T(8,128)(2,1)S(1)} %get-tuple-element.145), channel_id=1, replica_groups=mesh['dp'=8,'tensor'=4] {'tensor'}, dimensions={0}, use_global_device_ids=true | all-gather | bytes 983040 | tf_op jit(solution)/shard_map/all_gather | solution.py:35
  592.0 17.4 %all_gather.87 = bf16[512,768]{1,0:T(8,128)(2,1)S(1)} all-gather(bf16[128,768]{1,0:T(8,128)(2,1)S(1)} %get-tuple-element.105), channel_id=1, replica_groups=mesh['dp'=8,'tensor'=4] {'tensor'}, dimensions={0}, use_global_device_ids=true | all-gather | bytes 983040 | tf_op jit(solution)/shard_map/all_gather | solution.py:35
  698.2 19.8 %reduce-scatter.47.cloned.1.call-done = bf16[128,768]{1,0:T(8,128)(2,1)} async-done(((bf16[512,768]{1,0:T(8,128)(2,1)}), bf16[128,768]{1,0:T(8,128)(2,1)}) %reduce-scatter.47.cloned.1.call-update) | async-done | bytes 196624 | tf_op jit(solution)/shard_map/reduce_scatter | solution.py:50
  718.0 25.0 %reduce-scatter.55.cloned.1.call-done = bf16[128,768]{1,0:T(8,128)(2,1)} async-done(((bf16[512,768]{1,0:T(8,128)(2,1)}), bf16[128,768]{1,0:T(8,128)(2,1)}) %reduce-scatter.55.cloned.1.call-update) | async-done | bytes 196624 | tf_op jit(solution)/shard_map/reduce_scatter | solution.py:50
  749.8 40.9 %all-reduce = (f32[768]{0:T(1024)}, f32[768]{0:T(1024)}, f32[2,768]{1,0:T(2,128)}, f32[768]{0:T(1024)}, f32[768]{0:T(1024)}, /*index=5*/f32[768]{0:T(1024)}, f32[3072]{0:T(1024)}, f32[768]{0:T(1024)}) all-reduce(f32[768]{0:T(1024)} %add_add_fusion.15, f32[768]{0:T(1024)} %add_add_fusion.14, ...), channel_id=1, replica_groups=mesh['dp'=8,'tensor'=4] {'dp','tensor'}, use_global_device_ids=true, to_apply=%region_64.65 | all-reduce | flops 9216 | bytes 73728 | tf_op jit(solution)/shard_map/psum | solution.py:221
  799.0 33.0 %reduce-scatter.57.cloned.1.call-done = f32[96,768]{1,0:T(8,128)} async-done(((f32[768,768]{1,0:T(8,128)}), f32[96,768]{1,0:T(8,128)}) %reduce-scatter.57.cloned.1.call-update) | async-done | bytes 294928 | tf_op jit(solution)/shard_map/reduce_scatter | solution.py:210
  832.0 46.0 %reduce-scatter.59.cloned.1.call-done = f32[768,96]{0,1:T(8,128)} async-done(((f32[768,768]{0,1:T(8,128)}), f32[768,96]{0,1:T(8,128)}) %reduce-scatter.59.cloned.1.call-update) | async-done | bytes 294928 | tf_op jit(solution)/shard_map/reduce_scatter | solution.py:211
  (717 shorter events, 280.7 us)
Async XLA Ops:
  8.0 74.4 %reduce-scatter.25.cloned.1.call-start = ((), (), s32[]{:S(2)}) async-start(), calls=%async_computation.20 | async-start | bytes 983040 | tf_op jit(solution)/shard_map/reduce_scatter | solution.py:39
  60.8 97.4 %reduce-scatter.33.cloned.1.call-start = ((), (), s32[]{:S(2)}) async-start(), calls=%async_computation.26 | async-start | bytes 983040 | tf_op jit(solution)/shard_map/reduce_scatter | solution.py:39
  108.2 92.9 %all-gather.7.cloned.1.call-start = ((), (), s32[]{:S(2)}) async-start(), calls=%async_computation.21 | async-start | bytes 1327104 | tf_op jit(solution)/shard_map/all_gather | solution.py:113
  108.7 99.1 %all-gather.9.cloned.1.call-start = ((), (), s32[]{:S(2)}) async-start(), calls=%async_computation.22 | async-start | bytes 1327104 | tf_op jit(solution)/shard_map/all_gather | solution.py:114
  109.3 233.2 %reduce-scatter.49.cloned.1.call-start = ((), (), s32[]{:S(2)}) async-start(), calls=%async_computation.34 | async-start | bytes 983040 | tf_op jit(solution)/shard_map/reduce_scatter | solution.py:50
  214.8 127.8 %reduce-scatter.41.cloned.1.call-start = ((), (), s32[]{:S(2)}) async-start(), calls=%async_computation.30 | async-start | bytes 983040 | tf_op jit(solution)/shard_map/reduce_scatter | solution.py:50
  248.5 94.0 %reduce-scatter.29.cloned.1.call-start = ((), (), s32[]{:S(2)}) async-start(), calls=%async_computation.24 | async-start | bytes 983040 | tf_op jit(solution)/shard_map/reduce_scatter | solution.py:39
  283.2 59.4 %reduce-scatter.37.cloned.1.call-start = ((), (), s32[]{:S(2)}) async-start(), calls=%async_computation.28 | async-start | bytes 983040 | tf_op jit(solution)/shard_map/reduce_scatter | solution.py:39
  289.6 77.9 %reduce-scatter.27.cloned.1.call-start = ((), (), s32[]{:S(2)}) async-start(), calls=%async_computation.23 | async-start | bytes 983040 | tf_op jit(solution)/shard_map/reduce_scatter | solution.py:39
  293.0 135.1 %reduce-scatter.35.cloned.1.call-start = ((), (), s32[]{:S(2)}) async-start(), calls=%async_computation.27 | async-start | bytes 983040 | tf_op jit(solution)/shard_map/reduce_scatter | solution.py:39
  342.5 146.7 %reduce-scatter.53.cloned.1.call-start = ((), (), s32[]{:S(2)}) async-start(), calls=%async_computation.36 | async-start | bytes 983040 | tf_op jit(solution)/shard_map/reduce_scatter | solution.py:50
  428.0 63.7 %reduce-scatter.45.cloned.1.call-start = ((), (), s32[]{:S(2)}) async-start(), calls=%async_computation.32 | async-start | bytes 983040 | tf_op jit(solution)/shard_map/reduce_scatter | solution.py:50
  468.9 47.9 %reduce-scatter.51.cloned.1.call-start = ((), (), s32[]{:S(2)}) async-start(), calls=%async_computation.35 | async-start | bytes 983040 | tf_op jit(solution)/shard_map/reduce_scatter | solution.py:50
  477.4 64.3 %reduce-scatter.31.cloned.1.call-start = ((), (), s32[]{:S(2)}) async-start(), calls=%async_computation.25 | async-start | bytes 983040 | tf_op jit(solution)/shard_map/reduce_scatter | solution.py:39
  480.7 85.9 %reduce-scatter.39.cloned.1.call-start = ((), (), s32[]{:S(2)}) async-start(), calls=%async_computation.29 | async-start | bytes 983040 | tf_op jit(solution)/shard_map/reduce_scatter | solution.py:39
  486.6 210.0 %reduce-scatter.63.cloned.1.call-start = ((), (), s32[]{:S(2)}) async-start(), calls=%async_computation.41 | async-start | bytes 884736
  631.3 66.9 %reduce-scatter.43.cloned.1.call-start = ((), (), s32[]{:S(2)}) async-start(), calls=%async_computation.31 | async-start | bytes 983040 | tf_op jit(solution)/shard_map/reduce_scatter | solution.py:50
  638.1 80.0 %reduce-scatter.47.cloned.1.call-start = ((), (), s32[]{:S(2)}) async-start(), calls=%async_computation.33 | async-start | bytes 983040 | tf_op jit(solution)/shard_map/reduce_scatter | solution.py:50
  646.1 96.9 %reduce-scatter.55.cloned.1.call-start = ((), (), s32[]{:S(2)}) async-start(), calls=%async_computation.37 | async-start | bytes 983040 | tf_op jit(solution)/shard_map/reduce_scatter | solution.py:50
  654.0 143.1 %reduce-scatter.61.cloned.1.call-start = ((), (), s32[]{:S(2)}) async-start(), calls=%async_computation.40 | async-start | bytes 2211840
  669.3 162.7 %reduce-scatter.57.cloned.1.call-start = ((), (), s32[]{:S(2)}) async-start(), calls=%async_computation.38 | async-start | bytes 2654208 | tf_op jit(solution)/shard_map/reduce_scatter | solution.py:210
  676.9 201.1 %reduce-scatter.59.cloned.1.call-start = ((), (), s32[]{:S(2)}) async-start(), calls=%async_computation.39 | async-start | bytes 2654208 | tf_op jit(solution)/shard_map/reduce_scatter | solution.py:211
  696.0 97.3 %copy-start.39 = (f32[128,768]{1,0:T(8,128)S(1)}, f32[128,768]{1,0:T(8,128)}, u32[]{:S(2)}) copy-start(f32[128,768]{1,0:T(8,128)} %copy-done.38) | copy-start | bytes 1179652
  696.0 97.3 %copy-start.41 = (f32[128,768]{1,0:T(8,128)S(1)}, f32[128,768]{1,0:T(8,128)}, u32[]{:S(2)}) copy-start(f32[128,768]{1,0:T(8,128)} %copy-done.40) | copy-start | bytes 1179652
  (236 other events, 2658.4 us)
Sparse Core Ops, SparseCore 0:
  60.9 21.5 reduce-scatter.24
  108.3 31.8 reduce-scatter.32
  214.9 30.3 reduce-scatter.48
  248.7 32.4 reduce-scatter.40
  283.4 29.5 reduce-scatter.28
  315.1 26.2 reduce-scatter.36
  343.7 23.7 reduce-scatter.26
  369.7 31.7 reduce-scatter.34
  428.2 29.1 reduce-scatter.52
  469.0 22.6 reduce-scatter.44
  494.0 22.6 reduce-scatter.50
  518.9 22.6 reduce-scatter.30
  543.9 22.6 reduce-scatter.38
Sparse Core Ops, SparseCore 1:
  110.5 23.2 all-gather.6
  135.6 23.8 all-gather.8
  631.4 35.4 reduce-scatter.62
  669.7 23.2 reduce-scatter.42
  695.4 22.6 reduce-scatter.46
  720.4 22.7 reduce-scatter.54
  746.3 39.5 reduce-scatter.60
  789.7 42.2 reduce-scatter.56
  835.8 42.2 reduce-scatter.58
where the time goes:
time: 895 us; the launch traced here: 886 us
  blocking collectives  405 us (45%)
  waiting for transfers between devices  239 us (27%)
  matrix products  116 us (13%)
  other arithmetic  64 us (7%)
  local copies, waits for them, and re-layouts  41 us (5%)
  between operations  18.4 us (2%)
    all_gather x8, blocking collectives, gather_rows(): return lax.all_gather(values_low, 'tensor', axis=0, tiled=True)  172 us
    all_gather x8, blocking collectives, gather_grads(): return lax.all_gather(values_low, 'tensor', axis=0, tiled=True)  171 us
    reduce_scatter x8, waiting for transfers between devices, rows_sum(): lax.psum_scatter(jnp.einsum(einsum_form, operand_left, operand_right, pre...  86.2 us
    reduce_scatter x8, waiting for transfers between devices, grads_sum(): lax.psum_scatter(jnp.einsum(einsum_form, operand_left, operand_right, pre...  72.5 us
    dot_general x36, matrix products, contract(): lax.dot_general(operand_left, operand_right, (((left_dim,), (right_dim,))...  56.3 us
    reduce_scatter x1, waiting for transfers between devices, body(): lax.psum_scatter(full_grads[3], 'dp', scatter_dimension=1, tiled=True)  46 us
    psum x1, blocking collectives, body(): lax.psum((qv_whole, up_whole, out_total, down_total, gain1_total, shift1_...  40.9 us
    unnamed x483, local copies, waits for them, and re-layouts  39.4 us
  transfers between devices with their start and end apart: 22, of which 10 were waited for; matrix products, arithmetic and copies ran while one was open for 19% of the time, Pallas kernels for 0%

commit v1 on v0

--- a/solution.py
+++ b/solution.py
@@ -6,6 +6,28 @@
 HD = 64
 epsilon = 1e-05
 masked_value = -1000000000.0
+
+
+def laid_out(blocks, dim):
+    shape = list(blocks.shape[1:])
+    shape[dim] *= blocks.shape[0]
+    return jnp.moveaxis(blocks, 0, dim).reshape(shape)
+
+
+def collect(value, axis, dim):
+    size = lax.axis_size(axis)
+    pairs = [(i, (i + 1) % size) for i in range(size)]
+    back = [(b, a) for a, b in pairs]
+    lower, upper = ([], [])
+    for step in range(size - 1):
+        if step % 2 == 0:
+            lower.append(lax.ppermute(lower[-1] if lower else value, axis, pairs))
+        else:
+            upper.append(lax.ppermute(upper[-1] if upper else value, axis, back))
+    blocks = jnp.stack([*lower[::-1], value, *upper])
+    shift = lax.axis_index(axis) - len(lower)
+    blocks = blocks[(jnp.arange(size) - shift) % size]
+    return laid_out(blocks, dim)
 
 
 def layer_norm(stream_values, scales, shifts):
@@ -28,7 +50,7 @@
 
 
 def gather_rows(values_low):
-    return lax.all_gather(values_low, "tensor", axis=0, tiled=True)
+    return collect(values_low, "tensor", 0)
 
 
 def gather_grads(values_low):

time: 895 us -> 864 us (0.965)
  blocking collectives: 405 us -> 222 us
  waiting for transfers between devices: 239 us -> 329 us
  starting transfers between devices: 1.49 us -> 30.2 us
  other arithmetic: 64 us -> 79.6 us
  local copies, waits for them, and re-layouts: 41 us -> 56.1 us
    all_gather x8 -> x0, blocking collectives: 172 us -> none  [gather_rows(): return lax.all_gather(values_low, 'tensor', axis=0, tiled=True)]
    ppermute x0 -> x24, waiting for transfers between devices: none -> 50.2 us  [the longest x16 44.9 us: collect(): lower.append(lax.ppermute(lower[-1] if lower else value, axis, pairs))]
    reduce_scatter x8, waiting for transfers between devices: 86.2 us -> 127 us  [rows_sum(): lax.psum_scatter(jnp.einsum(einsum_form, operand_left, operand_right, pre...]
    ppermute x0 -> x24, starting transfers between devices: none -> 27.9 us  [the longest x8 22.1 us: collect(): upper.append(lax.ppermute(upper[-1] if upper else value, axis, back))]
    gather x0 -> x8, local copies, waits for them, and re-layouts: none -> 16.3 us  [collect(): blocks = blocks[(jnp.arange(size) - shift) % size]]
    another operation x0 -> x8, other arithmetic: none -> 12.8 us  [collect(): blocks = jnp.stack([*lower[::-1], value, *upper])]
    all_gather x8, blocking collectives: 171 us -> 160 us  [gather_grads(): return lax.all_gather(values_low, 'tensor', axis=0, tiled=True)]
  transfers between devices with their start and end apart: 22 -> 46, of which waited for: 10 -> 21; matrix products, arithmetic and copies ran while one was open for 19% -> 24% of each run, Pallas kernels for 0% -> 0%
where the time goes in v1:
time: 864 us; the launch traced here: 853 us
  waiting for transfers between devices  329 us (38%)
  blocking collectives  222 us (26%)
  matrix products  117 us (14%)
  other arithmetic  79.6 us (9%)
  local copies, waits for them, and re-layouts  56.1 us (6%)
  starting transfers between devices  30.2 us (3%)
  between operations  18.6 us (2%)
    all_gather x8, blocking collectives, gather_grads(): return lax.all_gather(values_low, 'tensor', axis=0, tiled=True)  160 us
    reduce_scatter x8, waiting for transfers between devices, rows_sum(): lax.psum_scatter(jnp.einsum(einsum_form, operand_left, operand_right, pre...  127 us
    reduce_scatter x8, waiting for transfers between devices, grads_sum(): lax.psum_scatter(jnp.einsum(einsum_form, operand_left, operand_right, pre...  71.5 us
    dot_general x36, matrix products, contract(): lax.dot_general(operand_left, operand_right, (((left_dim,), (right_dim,))...  57.3 us
    reduce_scatter x1, waiting for transfers between devices, body(): lax.psum_scatter(full_grads[3], 'dp', scatter_dimension=1, tiled=True)  46 us
    ppermute x16, waiting for transfers between devices, collect(): lower.append(lax.ppermute(lower[-1] if lower else value, axis, pairs))  44.9 us
    psum x1, blocking collectives, body(): lax.psum((qv_whole, up_whole, out_total, down_total, gain1_total, shift1_...  41 us
    unnamed x483, local copies, waits for them, and re-layouts  38.2 us
  transfers between devices with their start and end apart: 46, of which 21 were waited for; matrix products, arithmetic and copies ran while one was open for 24% of the time, Pallas kernels for 0%

profile of v1, /device:TPU:0, one launch (start us, length us, event | category | flops | bytes accessed | tf_op | source)
XLA Modules:
  0.0 853.0 jit_solution(8556266020117065071)
XLA Ops:
  18.6 7.7 collective-permute-done
  27.9 9.6 %all_gather.49 = bf16[192,768]{0,1:T(8,128)(2,1)S(1)} all-gather(bf16[192,96]{0,1:T(8,128)(2,1)S(1)} %copy.47), channel_id=1, replica_groups=mesh['dp'=8,'tensor'=4] {'dp'}, dimensions={1}, use_global_device_ids=true | all-gather | bytes 331776 | tf_op jit(solution)/shard_map/all_gather | solution.py:134
  37.4 11.7 %all_gather.48 = bf16[3,768,192]{2,1,0:T(8,128)(2,1)S(1)} all-gather(bf16[3,96,192]{2,1,0:T(8,128)(2,1)S(1)} %copy-done.133), channel_id=1, replica_groups=mesh['dp'=8,'tensor'=4] {'dp'}, dimensions={1}, use_global_device_ids=true | all-gather | bytes 995328 | tf_op jit(solution)/shard_map/all_gather | solution.py:133
  56.4 22.1 %reduce-scatter.25.cloned.1.call-done = bf16[128,768]{1,0:T(8,128)(2,1)} async-done(((bf16[512,768]{1,0:T(8,128)(2,1)}), bf16[128,768]{1,0:T(8,128)(2,1)}) %reduce-scatter.25.cloned.1.call-update) | async-done | bytes 196624 | tf_op jit(solution)/shard_map/reduce_scatter | solution.py:61
  108.3 27.9 %all-gather.2 = bf16[1,512,768]{2,1,0:T(8,128)(2,1)} all-gather(bf16[1,128,768]{2,1,0:T(8,128)(2,1)S(1)} %get-tuple-element.153), channel_id=4, replica_groups=mesh['dp'=8,'tensor'=4] {'tensor'}, dimensions={1}, use_global_device_ids=true | all-gather | bytes 983040 | tf_op jit(solution)/shard_map/all_gather | solution.py:57
  136.3 17.2 %all-gather = bf16[1,512,768]{2,1,0:T(8,128)(2,1)} all-gather(bf16[1,128,768]{2,1,0:T(8,128)(2,1)S(1)} %get-tuple-element.151), channel_id=2, replica_groups=mesh['dp'=8,'tensor'=4] {'tensor'}, dimensions={1}, use_global_device_ids=true | all-gather | bytes 983040 | tf_op jit(solution)/shard_map/all_gather | solution.py:57
  175.5 10.7 %collective-permute-done.6 = bf16[128,768]{1,0:T(8,128)(2,1)S(1)} collective-permute-done((bf16[128,768]{1,0:T(8,128)(2,1)}, bf16[128,768]{1,0:T(8,128)(2,1)S(1)}, u32[]{:S(2)}, u32[]{:S(2)}) %collective-permute-start.6) | collective-permute-done | bytes 196640 | tf_op jit(solution)/shard_map/ppermute | solution.py:24
  257.7 24.4 %all-gather.3 = bf16[1,512,768]{2,1,0:T(8,128)(2,1)} all-gather(bf16[1,128,768]{2,1,0:T(8,128)(2,1)S(1)} %copy-done.105), channel_id=5, replica_groups=mesh['dp'=8,'tensor'=4] {'tensor'}, dimensions={1}, use_global_device_ids=true | all-gather | bytes 983040 | tf_op jit(solution)/shard_map/all_gather | solution.py:57
  282.1 19.5 %all-gather.1 = bf16[1,512,768]{2,1,0:T(8,128)(2,1)} all-gather(bf16[1,128,768]{2,1,0:T(8,128)(2,1)S(1)} %copy-done.104), channel_id=3, replica_groups=mesh['dp'=8,'tensor'=4] {'tensor'}, dimensions={1}, use_global_device_ids=true | all-gather | bytes 983040 | tf_op jit(solution)/shard_map/all_gather | solution.py:57
  304.2 14.1 %reduce-scatter.37.cloned.1.call-done = bf16[128,768]{1,0:T(8,128)(2,1)} async-done(((bf16[512,768]{1,0:T(8,128)(2,1)}), bf16[128,768]{1,0:T(8,128)(2,1)}) %reduce-scatter.37.cloned.1.call-update) | async-done | bytes 196624 | tf_op jit(solution)/shard_map/reduce_scatter | solution.py:61
  323.0 20.3 %reduce-scatter.27.cloned.1.call-done = bf16[128,768]{1,0:T(8,128)(2,1)} async-done(((bf16[512,768]{1,0:T(8,128)(2,1)}), bf16[128,768]{1,0:T(8,128)(2,1)}) %reduce-scatter.27.cloned.1.call-update) | async-done | bytes 196624 | tf_op jit(solution)/shard_map/reduce_scatter | solution.py:61
  353.6 25.7 %reduce-scatter.35.cloned.1.call-done = bf16[128,768]{1,0:T(8,128)(2,1)} async-done(((bf16[512,768]{1,0:T(8,128)(2,1)}), bf16[128,768]{1,0:T(8,128)(2,1)}) %reduce-scatter.35.cloned.1.call-update) | async-done | bytes 196624 | tf_op jit(solution)/shard_map/reduce_scatter | solution.py:61
  383.4 18.3 %all_gather.57 = bf16[512,768]{1,0:T(8,128)(2,1)S(1)} all-gather(bf16[128,768]{1,0:T(8,128)(2,1)S(1)} %get-tuple-element.109), channel_id=1, replica_groups=mesh['dp'=8,'tensor'=4] {'tensor'}, dimensions={0}, use_global_device_ids=true | all-gather | bytes 983040 | tf_op jit(solution)/shard_map/all_gather | solution.py:57
  459.3 25.0 %reduce-scatter.45.cloned.1.call-done = bf16[128,768]{1,0:T(8,128)(2,1)} async-done(((bf16[512,768]{1,0:T(8,128)(2,1)}), bf16[128,768]{1,0:T(8,128)(2,1)}) %reduce-scatter.45.cloned.1.call-update) | async-done | bytes 196624 | tf_op jit(solution)/shard_map/reduce_scatter | solution.py:72
  487.1 22.0 %reduce-scatter.31.cloned.1.call-done = bf16[128,768]{1,0:T(8,128)(2,1)} async-done(((bf16[512,768]{1,0:T(8,128)(2,1)}), bf16[128,768]{1,0:T(8,128)(2,1)}) %reduce-scatter.31.cloned.1.call-update) | async-done | bytes 196624 | tf_op jit(solution)/shard_map/reduce_scatter | solution.py:61
  511.3 22.8 %reduce-scatter.39.cloned.1.call-done = bf16[128,768]{1,0:T(8,128)(2,1)} async-done(((bf16[512,768]{1,0:T(8,128)(2,1)}), bf16[128,768]{1,0:T(8,128)(2,1)}) %reduce-scatter.39.cloned.1.call-update) | async-done | bytes 196624 | tf_op jit(solution)/shard_map/reduce_scatter | solution.py:61
  537.2 18.0 %all_gather.53 = bf16[512,768]{1,0:T(8,128)(2,1)S(1)} all-gather(bf16[128,768]{1,0:T(8,128)(2,1)S(1)} %get-tuple-element.147), channel_id=1, replica_groups=mesh['dp'=8,'tensor'=4] {'tensor'}, dimensions={0}, use_global_device_ids=true | all-gather | bytes 983040 | tf_op jit(solution)/shard_map/all_gather | solution.py:57
  559.1 17.5 %all_gather.55 = bf16[512,768]{1,0:T(8,128)(2,1)S(1)} all-gather(bf16[128,768]{1,0:T(8,128)(2,1)S(1)} %get-tuple-element.105), channel_id=1, replica_groups=mesh['dp'=8,'tensor'=4] {'tensor'}, dimensions={0}, use_global_device_ids=true | all-gather | bytes 983040 | tf_op jit(solution)/shard_map/all_gather | solution.py:57
  576.6 17.1 %all_gather.59 = bf16[512,768]{1,0:T(8,128)(2,1)S(1)} all-gather(bf16[128,768]{1,0:T(8,128)(2,1)S(1)} %get-tuple-element.149), channel_id=1, replica_groups=mesh['dp'=8,'tensor'=4] {'tensor'}, dimensions={0}, use_global_device_ids=true | all-gather | bytes 983040 | tf_op jit(solution)/shard_map/all_gather | solution.py:57
  664.2 21.5 %reduce-scatter.47.cloned.1.call-done = bf16[128,768]{1,0:T(8,128)(2,1)} async-done(((bf16[512,768]{1,0:T(8,128)(2,1)}), bf16[128,768]{1,0:T(8,128)(2,1)}) %reduce-scatter.47.cloned.1.call-update) | async-done | bytes 196624 | tf_op jit(solution)/shard_map/reduce_scatter | solution.py:72
  685.6 25.0 %reduce-scatter.55.cloned.1.call-done = bf16[128,768]{1,0:T(8,128)(2,1)} async-done(((bf16[512,768]{1,0:T(8,128)(2,1)}), bf16[128,768]{1,0:T(8,128)(2,1)}) %reduce-scatter.55.cloned.1.call-update) | async-done | bytes 196624 | tf_op jit(solution)/shard_map/reduce_scatter | solution.py:72
  717.4 41.0 %all-reduce = (f32[768]{0:T(1024)}, f32[768]{0:T(1024)}, f32[2,768]{1,0:T(2,128)}, f32[768]{0:T(1024)}, f32[768]{0:T(1024)}, /*index=5*/f32[768]{0:T(1024)}, f32[3072]{0:T(1024)}, f32[768]{0:T(1024)}) all-reduce(f32[768]{0:T(1024)} %add_add_fusion.15, f32[768]{0:T(1024)} %add_add_fusion.14, ...), channel_id=1, replica_groups=mesh['dp'=8,'tensor'=4] {'dp','tensor'}, use_global_device_ids=true, to_apply=%region_64.65 | all-reduce | flops 9216 | bytes 73728 | tf_op jit(solution)/shard_map/psum | solution.py:243
  766.6 32.8 %reduce-scatter.57.cloned.1.call-done = f32[96,768]{1,0:T(8,128)} async-done(((f32[768,768]{1,0:T(8,128)}), f32[96,768]{1,0:T(8,128)}) %reduce-scatter.57.cloned.1.call-update) | async-done | bytes 294928 | tf_op jit(solution)/shard_map/reduce_scatter | solution.py:232
  799.4 46.0 %reduce-scatter.59.cloned.1.call-done = f32[768,96]{0,1:T(8,128)} async-done(((f32[768,768]{0,1:T(8,128)}), f32[768,96]{0,1:T(8,128)}) %reduce-scatter.59.cloned.1.call-update) | async-done | bytes 294928 | tf_op jit(solution)/shard_map/reduce_scatter | solution.py:233
  (778 shorter events, 316.4 us)
Async XLA Ops:
  8.1 70.5 %reduce-scatter.25.cloned.1.call-start = ((), (), s32[]{:S(2)}) async-start(), calls=%async_computation.20 | async-start | bytes 983040 | tf_op jit(solution)/shard_map/reduce_scatter | solution.py:61
  56.3 98.1 %reduce-scatter.33.cloned.1.call-start = ((), (), s32[]{:S(2)}) async-start(), calls=%async_computation.26 | async-start | bytes 983040 | tf_op jit(solution)/shard_map/reduce_scatter | solution.py:61
  106.3 85.3 %all-gather.7.cloned.1.call-start = ((), (), s32[]{:S(2)}) async-start(), calls=%async_computation.21 | async-start | bytes 1327104 | tf_op jit(solution)/shard_map/all_gather | solution.py:135
  106.9 91.5 %all-gather.9.cloned.1.call-start = ((), (), s32[]{:S(2)}) async-start(), calls=%async_computation.22 | async-start | bytes 1327104 | tf_op jit(solution)/shard_map/all_gather | solution.py:136
  107.5 196.6 %reduce-scatter.49.cloned.1.call-start = ((), (), s32[]{:S(2)}) async-start(), calls=%async_computation.34 | async-start | bytes 983040 | tf_op jit(solution)/shard_map/reduce_scatter | solution.py:72
  204.4 99.7 %reduce-scatter.41.cloned.1.call-start = ((), (), s32[]{:S(2)}) async-start(), calls=%async_computation.30 | async-start | bytes 983040 | tf_op jit(solution)/shard_map/reduce_scatter | solution.py:72
  233.3 70.8 %reduce-scatter.29.cloned.1.call-start = ((), (), s32[]{:S(2)}) async-start(), calls=%async_computation.24 | async-start | bytes 983040 | tf_op jit(solution)/shard_map/reduce_scatter | solution.py:61
  247.7 70.6 %reduce-scatter.37.cloned.1.call-start = ((), (), s32[]{:S(2)}) async-start(), calls=%async_computation.28 | async-start | bytes 983040 | tf_op jit(solution)/shard_map/reduce_scatter | solution.py:61
  253.9 89.4 %reduce-scatter.27.cloned.1.call-start = ((), (), s32[]{:S(2)}) async-start(), calls=%async_computation.23 | async-start | bytes 983040 | tf_op jit(solution)/shard_map/reduce_scatter | solution.py:61
  257.6 121.8 %reduce-scatter.35.cloned.1.call-start = ((), (), s32[]{:S(2)}) async-start(), calls=%async_computation.27 | async-start | bytes 983040 | tf_op jit(solution)/shard_map/reduce_scatter | solution.py:61
  304.0 155.2 %reduce-scatter.51.cloned.1.call-start = ((), (), s32[]{:S(2)}) async-start(), calls=%async_computation.35 | async-start | bytes 983040 | tf_op jit(solution)/shard_map/reduce_scatter | solution.py:72
  347.4 62.9 %collective-permute-start.23 = (bf16[128,768]{1,0:T(8,128)(2,1)}, bf16[128,768]{1,0:T(8,128)(2,1)}, u32[]{:S(2)}, u32[]{:S(2)}) collective-permute-start(bf16[128,768]{1,0:T(8,128)(2,1)} %get-tuple-element.137), channel_id=1, source_target_pairs={{1,0},{2,1},{3,2},{0,3},{5,4},{6,5},{7,6},{4,7},{9,8},{10,9},{11,1... | collective-permute-start | bytes 589832 | tf_op jit(solution)/shard_map/ppermute | solution.py:26
  349.3 57.6 %collective-permute-start.21 = (bf16[128,768]{1,0:T(8,128)(2,1)}, bf16[128,768]{1,0:T(8,128)(2,1)}, u32[]{:S(2)}, u32[]{:S(2)}) collective-permute-start(bf16[128,768]{1,0:T(8,128)(2,1)} %get-tuple-element.137), channel_id=1, source_target_pairs={{0,1},{1,2},{2,3},{3,0},{4,5},{5,6},{6,7},{7,4},{8,9},{9,10},{10,1... | collective-permute-start | bytes 589832 | tf_op jit(solution)/shard_map/ppermute | solution.py:24
  349.4 70.9 %collective-permute-start.11 = (bf16[128,768]{1,0:T(8,128)(2,1)}, bf16[128,768]{1,0:T(8,128)(2,1)}, u32[]{:S(2)}, u32[]{:S(2)}) collective-permute-start(bf16[128,768]{1,0:T(8,128)(2,1)} %get-tuple-element.136), channel_id=1, source_target_pairs={{1,0},{2,1},{3,2},{0,3},{5,4},{6,5},{7,6},{4,7},{9,8},{10,9},{11,1... | collective-permute-start | bytes 589832 | tf_op jit(solution)/shard_map/ppermute | solution.py:26
  353.1 53.8 %collective-permute-start.9 = (bf16[128,768]{1,0:T(8,128)(2,1)}, bf16[128,768]{1,0:T(8,128)(2,1)}, u32[]{:S(2)}, u32[]{:S(2)}) collective-permute-start(bf16[128,768]{1,0:T(8,128)(2,1)} %get-tuple-element.136), channel_id=1, source_target_pairs={{0,1},{1,2},{2,3},{3,0},{4,5},{5,6},{6,7},{7,4},{8,9},{9,10},{10,1... | collective-permute-start | bytes 589832 | tf_op jit(solution)/shard_map/ppermute | solution.py:24
  447.1 62.0 %reduce-scatter.31.cloned.1.call-start = ((), (), s32[]{:S(2)}) async-start(), calls=%async_computation.25 | async-start | bytes 983040 | tf_op jit(solution)/shard_map/reduce_scatter | solution.py:61
  450.7 83.5 %reduce-scatter.39.cloned.1.call-start = ((), (), s32[]{:S(2)}) async-start(), calls=%async_computation.29 | async-start | bytes 983040 | tf_op jit(solution)/shard_map/reduce_scatter | solution.py:61
  456.6 205.9 %reduce-scatter.63.cloned.1.call-start = ((), (), s32[]{:S(2)}) async-start(), calls=%async_computation.41 | async-start | bytes 884736
  598.5 65.7 %reduce-scatter.43.cloned.1.call-start = ((), (), s32[]{:S(2)}) async-start(), calls=%async_computation.31 | async-start | bytes 983040 | tf_op jit(solution)/shard_map/reduce_scatter | solution.py:72
  605.3 80.4 %reduce-scatter.47.cloned.1.call-start = ((), (), s32[]{:S(2)}) async-start(), calls=%async_computation.33 | async-start | bytes 983040 | tf_op jit(solution)/shard_map/reduce_scatter | solution.py:72
  613.7 96.9 %reduce-scatter.55.cloned.1.call-start = ((), (), s32[]{:S(2)}) async-start(), calls=%async_computation.37 | async-start | bytes 983040 | tf_op jit(solution)/shard_map/reduce_scatter | solution.py:72
  621.3 143.4 %reduce-scatter.61.cloned.1.call-start = ((), (), s32[]{:S(2)}) async-start(), calls=%async_computation.40 | async-start | bytes 2211840
  636.2 163.2 %reduce-scatter.57.cloned.1.call-start = ((), (), s32[]{:S(2)}) async-start(), calls=%async_computation.38 | async-start | bytes 2654208 | tf_op jit(solution)/shard_map/reduce_scatter | solution.py:232
  643.8 201.6 %reduce-scatter.59.cloned.1.call-start = ((), (), s32[]{:S(2)}) async-start(), calls=%async_computation.39 | async-start | bytes 2654208 | tf_op jit(solution)/shard_map/reduce_scatter | solution.py:233
  (260 other events, 3239.8 us)
Sparse Core Ops, SparseCore 0:
  56.4 22.0 reduce-scatter.24
  106.4 31.0 reduce-scatter.32
  204.5 27.0 reduce-scatter.48
  233.7 25.7 reduce-scatter.40
  261.7 31.2 reduce-scatter.28
  295.2 22.9 reduce-scatter.36
  320.5 22.6 reduce-scatter.26
  345.6 33.7 reduce-scatter.34
  410.2 23.6 reduce-scatter.50
  436.6 22.6 reduce-scatter.52
  461.6 22.6 reduce-scatter.44
  486.4 22.6 reduce-scatter.30
  511.4 22.6 reduce-scatter.38
Sparse Core Ops, SparseCore 1:
  108.6 21.9 all-gather.6
  132.4 23.8 all-gather.8
  598.5 35.8 reduce-scatter.62
  637.3 23.2 reduce-scatter.42
  662.9 22.7 reduce-scatter.46
  687.9 22.6 reduce-scatter.54
  713.9 39.5 reduce-scatter.60
  757.2 42.1 reduce-scatter.56
  803.2 42.2 reduce-scatter.58
